TPU v7x, 32 devices: a whole 2x2x4 slice. The times are simulated.
32 devices in a mesh: row: 4 (over z), col: 8 (over y, x, core).
Axes of the slice: x: 2, y: 2, z: 4, core: 2. Of those that a mesh axis runs over, the one named last changes fastest.
Arguments:
- factor_wide: float32 [4, 4, 2, 8, 512, 512], P(None, 'row', None, 'col'), may hold values from -1 to 2, as said below
- factor_narrow: bfloat16 [4, 4, 2, 8, 512, 512], P(None, 'row', None, 'col'), may hold values from -1 to 2, as said below
- flags: int32 [4, 4, 2, 8], P(None, 'row', None, 'col'), may hold values from 0 to 1
- forward_solution: float32 [2, 8, 512, 128], P(None, 'col'), may hold values from -0.5 to 0.5
- solution_grad: float32 [2, 8, 512, 128], P(None, 'col'), may hold values from -1.8 to 1.8
Outputs:
- rhs_grad: float32 [4, 4, 512, 128], P(None, 'row')
- factor_grad: float32 [4, 4, 2, 8, 512, 512], P(None, 'row', None, 'col')
Inputs may be any that keep to these rules, and one draw needn't show every extreme that they name: `factor_wide`: the diagonal entries of every diagonal tile lie between 1 and 2. `factor_narrow`: the diagonal entries of every diagonal tile lie between 1 and 2.
All inputs are finite; a program needn't handle non-finite values.
Results may differ from a plain program's by a relative error of at most 0.0003.
Values sent between devices are 32-bit elements; how exact they have to be, the bound alone decides.
A program may use at most 64 MiB of HBM per device.

v0:
```python
import jax
import jax.numpy as jnp
from jax import lax
from jax.sharding import PartitionSpec as P

HIGHEST_PRECISION = lax.Precision.HIGHEST


def broadcast(value, axis, root):
    mine = lax.axis_index(axis) == root
    return lax.psum(jnp.where(mine, value, jnp.zeros_like(value)), axis)


def from_behind(value, axis, by):
    size = lax.axis_size(axis)
    return lax.ppermute(value, axis, [(i, (i + by) % size) for i in range(size)])


def lower_mask(row_index, col_index, tile_width):
    inner_mask = lax.broadcasted_iota(
        jnp.int32, (tile_width, tile_width), 0
    ) >= lax.broadcasted_iota(jnp.int32, (tile_width, tile_width), 1)
    return (row_index > col_index) | (row_index == col_index) & inner_mask


def body(factor_wide, factor_narrow, flags, forward_solution, solution_grad):
    row_count = lax.axis_size("row")
    col_count = lax.axis_size("col")
    my_row = lax.axis_index("row")
    my_col = lax.axis_index("col")
    local_rows = factor_wide.shape[0]
    local_cols = factor_wide.shape[2]
    tile_width = factor_wide.shape[4]
    rhs_width = forward_solution.shape[3]
    tile_count = local_rows * row_count
    factor_tiles = jnp.where(
        flags[:, 0, :, 0, None, None] == 1,
        factor_narrow[:, 0, :, 0].astype(jnp.float32),
        factor_wide[:, 0, :, 0],
    )
    solution_local = forward_solution[:, 0]
    target_local = solution_grad[:, 0]
    row_index = jnp.arange(local_rows, dtype=jnp.int32) * row_count + my_row
    col_index = jnp.arange(local_cols, dtype=jnp.int32) * col_count + my_col
    empty_block = jnp.zeros((tile_width, rhs_width), jnp.float32)

    def nothing_block():
        return empty_block

    def column_partial(rhs_local, target, lowest):

        def on_owner():
            column = lax.dynamic_index_in_dim(factor_tiles, target // col_count, 1, keepdims=False)
            weight = (row_index >= lowest).astype(jnp.float32)
            masked = rhs_local * weight[:, None, None]
            return jnp.einsum("aki,akr->ir", column, masked, precision=HIGHEST_PRECISION)

        return lax.cond(my_col == target % col_count, on_owner, nothing_block)

    def target_block(target):
        return lax.dynamic_index_in_dim(target_local, target // col_count, 0, keepdims=False)

    def advance(right_side, target, carried):
        rhs_local, factor_grad = carried
        local_slot = target // row_count
        holds_row = my_row == target % row_count
        is_owner = holds_row & (my_col == target % col_count)

        def solve_here():
            tile_row = lax.dynamic_index_in_dim(factor_tiles, local_slot, 0, keepdims=False)
            diagonal = lax.dynamic_index_in_dim(tile_row, target // col_count, 0, keepdims=False)
            return lax.linalg.triangular_solve(
                diagonal, right_side, left_side=True, lower=True, transpose_a=True
            )

        solved = lax.cond(is_owner, solve_here, nothing_block)
        arrived = broadcast(solved, "col", target % col_count)
        current = lax.dynamic_index_in_dim(rhs_local, local_slot, 0, keepdims=False)
        rhs_local = lax.dynamic_update_index_in_dim(
            rhs_local, jnp.where(holds_row, arrived, current), local_slot, 0
        )
        return (rhs_local, factor_grad)

    final_index = tile_count - 1
    carried = (
        jnp.zeros((local_rows, tile_width, rhs_width), jnp.float32),
        jnp.zeros((local_rows, local_cols, tile_width, tile_width), jnp.float32),
    )
    carried = advance(target_block(jnp.int32(final_index)), jnp.int32(final_index), carried)

    def sweep_step(offset, loop_state):
        carried, early_sum = loop_state
        target = final_index - 1 - offset
        rhs_local = carried[0]
        source = target + 1

        def compute_fresh():
            tile_row = lax.dynamic_index_in_dim(
                factor_tiles, source // row_count, 0, keepdims=False
            )
            tile_now = lax.dynamic_index_in_dim(tile_row, target // col_count, 0, keepdims=False)
            newest = lax.dynamic_index_in_dim(rhs_local, source // row_count, 0, keepdims=False)
            return jnp.dot(
                tile_now.T, newest, precision=HIGHEST_PRECISION, preferred_element_type=jnp.float32
            )

        fresh_owner = (my_row == source % row_count) & (my_col == target % col_count)
        fresh_term = lax.cond(fresh_owner, compute_fresh, nothing_block)
        moved_term = from_behind(fresh_term, "row", -1)
        following = jnp.maximum(target - 1, 0)
        next_partial = column_partial(rhs_local, following, source)
        next_sum = lax.psum(next_partial, "row")
        carried = advance(target_block(target) - early_sum - moved_term, target, carried)
        return (carried, next_sum)

    carried, unused_sum = lax.fori_loop(0, final_index, sweep_step, (carried, empty_block))
    rhs_local, factor_grad = carried
    products = -jnp.einsum("akr,blr->abkl", rhs_local, solution_local, precision=HIGHEST_PRECISION)
    masks = lower_mask(row_index[:, None, None, None], col_index[None, :, None, None], tile_width)
    factor_grad = jnp.where(masks, products, jnp.zeros_like(products))
    return (rhs_local[:, None], factor_grad[:, None, :, None])


def solution(mesh):
    placed = (
        P(None, "row", None, "col", None, None),
        P(None, "row", None, "col", None, None),
        P(None, "row", None, "col"),
        P(None, "col", None, None),
        P(None, "col", None, None),
    )
    return jax.shard_map(
        body,
        mesh=mesh,
        in_specs=placed,
        out_specs=(P(None, "row", None, None), P(None, "row", None, "col", None, None)),
        check_vma=False,
    )
```

profile of v0, /device:TPU:0, one launch (start us, length us, event | category | flops | bytes accessed | tf_op | source)
XLA Modules:
  0.0 2219.2 jit_solution(8826648313586827079)
XLA Ops:
  7.3 9.9 copy.12
  17.2 7.3 copy.11
  24.5 9.6 convert_select_fusion
  35.9 117.2 %all-reduce.5.cloned.1.call-done = f32[512,128]{1,0:T(8,128)} async-done(((f32[512,128]{1,0:T(8,128)}), f32[512,128]{1,0:T(8,128)}) %all-reduce.5.cloned.1.call-update) | async-done | bytes 262160 | tf_op jit(solution)/shard_map/psum | solution.py:11
  153.2 2048.1 %while.28 = (s32[]{:T(128)}, f32[4,512,128]{2,1,0:T(8,128)S(1)}, f32[512,128]{1,0:T(8,128)S(1)}, s32[]{:T(128)}, s32[]{:T(128)}, /*index=5*/f32[4,2,512,512]{2,3...) while((s32[]{:T(128)}, f32[4,512,128]{2,1,0:T(8,128)S(1)}, ...), condition=%wide.region_12.14_spmd.clone.clone, body=%wide.region_3.13_spmd.clone.clone.sunk | while | flops 2266480640 | bytes 54005560 | solution.py:116
  163.3 40.6 %all-reduce.9.cloned.1.call-done = f32[512,128]{1,0:T(8,128)} async-done(((f32[512,128]{1,0:T(8,128)}), f32[512,128]{1,0:T(8,128)}) %all-reduce.9.cloned.1.call-update) | async-done | bytes 262160 | tf_op jit(solution)/shard_map/while/body/eval_jaxpr/psum | solution.py:112
  204.9 86.8 %all-reduce.7.cloned.1.call-done = f32[512,128]{1,0:T(8,128)} async-done(((f32[512,128]{1,0:T(8,128)}), f32[512,128]{1,0:T(8,128)}) %all-reduce.7.cloned.1.call-update) | async-done | bytes 262160 | tf_op jit(solution)/shard_map/while/body/eval_jaxpr/psum | solution.py:11
  300.8 39.6 %all-reduce.9.cloned.1.call-done = f32[512,128]{1,0:T(8,128)} async-done(((f32[512,128]{1,0:T(8,128)}), f32[512,128]{1,0:T(8,128)}) %all-reduce.9.cloned.1.call-update) | async-done | bytes 262160 | tf_op jit(solution)/shard_map/while/body/eval_jaxpr/psum | solution.py:112
  341.4 85.4 %all-reduce.7.cloned.1.call-done = f32[512,128]{1,0:T(8,128)} async-done(((f32[512,128]{1,0:T(8,128)}), f32[512,128]{1,0:T(8,128)}) %all-reduce.7.cloned.1.call-update) | async-done | bytes 262160 | tf_op jit(solution)/shard_map/while/body/eval_jaxpr/psum | solution.py:11
  435.9 40.6 %all-reduce.9.cloned.1.call-done = f32[512,128]{1,0:T(8,128)} async-done(((f32[512,128]{1,0:T(8,128)}), f32[512,128]{1,0:T(8,128)}) %all-reduce.9.cloned.1.call-update) | async-done | bytes 262160 | tf_op jit(solution)/shard_map/while/body/eval_jaxpr/psum | solution.py:112
  477.4 85.9 %all-reduce.7.cloned.1.call-done = f32[512,128]{1,0:T(8,128)} async-done(((f32[512,128]{1,0:T(8,128)}), f32[512,128]{1,0:T(8,128)}) %all-reduce.7.cloned.1.call-update) | async-done | bytes 262160 | tf_op jit(solution)/shard_map/while/body/eval_jaxpr/psum | solution.py:11
  572.6 37.7 %all-reduce.9.cloned.1.call-done = f32[512,128]{1,0:T(8,128)} async-done(((f32[512,128]{1,0:T(8,128)}), f32[512,128]{1,0:T(8,128)}) %all-reduce.9.cloned.1.call-update) | async-done | bytes 262160 | tf_op jit(solution)/shard_map/while/body/eval_jaxpr/psum | solution.py:112
  611.3 88.0 %all-reduce.7.cloned.1.call-done = f32[512,128]{1,0:T(8,128)} async-done(((f32[512,128]{1,0:T(8,128)}), f32[512,128]{1,0:T(8,128)}) %all-reduce.7.cloned.1.call-update) | async-done | bytes 262160 | tf_op jit(solution)/shard_map/while/body/eval_jaxpr/psum | solution.py:11
  709.4 40.6 %all-reduce.9.cloned.1.call-done = f32[512,128]{1,0:T(8,128)} async-done(((f32[512,128]{1,0:T(8,128)}), f32[512,128]{1,0:T(8,128)}) %all-reduce.9.cloned.1.call-update) | async-done | bytes 262160 | tf_op jit(solution)/shard_map/while/body/eval_jaxpr/psum | solution.py:112
  751.0 86.8 %all-reduce.7.cloned.1.call-done = f32[512,128]{1,0:T(8,128)} async-done(((f32[512,128]{1,0:T(8,128)}), f32[512,128]{1,0:T(8,128)}) %all-reduce.7.cloned.1.call-update) | async-done | bytes 262160 | tf_op jit(solution)/shard_map/while/body/eval_jaxpr/psum | solution.py:11
  841.4 5.7 conditional.16
  841.4 5.7 fusion.11
  848.8 37.8 %all-reduce.9.cloned.1.call-done = f32[512,128]{1,0:T(8,128)} async-done(((f32[512,128]{1,0:T(8,128)}), f32[512,128]{1,0:T(8,128)}) %all-reduce.9.cloned.1.call-update) | async-done | bytes 262160 | tf_op jit(solution)/shard_map/while/body/eval_jaxpr/psum | solution.py:112
  887.5 85.3 %all-reduce.7.cloned.1.call-done = f32[512,128]{1,0:T(8,128)} async-done(((f32[512,128]{1,0:T(8,128)}), f32[512,128]{1,0:T(8,128)}) %all-reduce.7.cloned.1.call-update) | async-done | bytes 262160 | tf_op jit(solution)/shard_map/while/body/eval_jaxpr/psum | solution.py:11
  977.3 15.6 collective-permute-done
  992.9 65.2 %conditional.15 = (f32[512,128]{1,0:T(8,128)S(1)}) conditional(s32[]{:T(128)} %convert_element_type.68, () %tuple.144, (s32[]{:T(128)}, s32[]{:T(128)}, f32[4,2,512,512]{2,3,0,1:T(8,128)}, s32[]{:T(128)}, pred[]{:T(512)}, /*index=5*/pred[]{:T(512)}, s32[]{:T(128)}, f32[2,512,128]{2,1,0:T(8,128)}, f32[512,128]{1,0:T(8,128)S(1)}, ...), branch_computations={%region_6.7_spmd, %region_7.8_spmd} | conditional | flops 252690464 | bytes 22546512 | solution.py:76
  992.9 10.0 copy.8
  1004.2 10.6 while.27
  1014.8 40.1 %custom-call.5 = f32[4,128,128]{1,2,0:T(8,128)S(1)} custom-call(f32[4,128,128]{2,1,0:T(8,128)} %get-tuple-element.560), custom_call_target="InvertDiagBlocksLowerTriangular" | custom-call | tf_op jit(solution)/shard_map/while/body/eval_jaxpr/cond/branch_1_fun/triangular_solve/custom-call.1 | solution.py:72
  1059.8 48.9 %all-reduce.7.cloned.1.call-done = f32[512,128]{1,0:T(8,128)} async-done(((f32[512,128]{1,0:T(8,128)}), f32[512,128]{1,0:T(8,128)}) %all-reduce.7.cloned.1.call-update) | async-done | bytes 262160 | tf_op jit(solution)/shard_map/while/body/eval_jaxpr/psum | solution.py:11
  1118.0 37.9 %all-reduce.9.cloned.1.call-done = f32[512,128]{1,0:T(8,128)} async-done(((f32[512,128]{1,0:T(8,128)}), f32[512,128]{1,0:T(8,128)}) %all-reduce.9.cloned.1.call-update) | async-done | bytes 262160 | tf_op jit(solution)/shard_map/while/body/eval_jaxpr/psum | solution.py:112
  1156.9 88.0 %all-reduce.7.cloned.1.call-done = f32[512,128]{1,0:T(8,128)} async-done(((f32[512,128]{1,0:T(8,128)}), f32[512,128]{1,0:T(8,128)}) %all-reduce.7.cloned.1.call-update) | async-done | bytes 262160 | tf_op jit(solution)/shard_map/while/body/eval_jaxpr/psum | solution.py:11
  1255.0 40.6 %all-reduce.9.cloned.1.call-done = f32[512,128]{1,0:T(8,128)} async-done(((f32[512,128]{1,0:T(8,128)}), f32[512,128]{1,0:T(8,128)}) %all-reduce.9.cloned.1.call-update) | async-done | bytes 262160 | tf_op jit(solution)/shard_map/while/body/eval_jaxpr/psum | solution.py:112
  1296.5 86.8 %all-reduce.7.cloned.1.call-done = f32[512,128]{1,0:T(8,128)} async-done(((f32[512,128]{1,0:T(8,128)}), f32[512,128]{1,0:T(8,128)}) %all-reduce.7.cloned.1.call-update) | async-done | bytes 262160 | tf_op jit(solution)/shard_map/while/body/eval_jaxpr/psum | solution.py:11
  1392.5 39.6 %all-reduce.9.cloned.1.call-done = f32[512,128]{1,0:T(8,128)} async-done(((f32[512,128]{1,0:T(8,128)}), f32[512,128]{1,0:T(8,128)}) %all-reduce.9.cloned.1.call-update) | async-done | bytes 262160 | tf_op jit(solution)/shard_map/while/body/eval_jaxpr/psum | solution.py:112
  1433.0 85.3 %all-reduce.7.cloned.1.call-done = f32[512,128]{1,0:T(8,128)} async-done(((f32[512,128]{1,0:T(8,128)}), f32[512,128]{1,0:T(8,128)}) %all-reduce.7.cloned.1.call-update) | async-done | bytes 262160 | tf_op jit(solution)/shard_map/while/body/eval_jaxpr/psum | solution.py:11
  1527.5 40.6 %all-reduce.9.cloned.1.call-done = f32[512,128]{1,0:T(8,128)} async-done(((f32[512,128]{1,0:T(8,128)}), f32[512,128]{1,0:T(8,128)}) %all-reduce.9.cloned.1.call-update) | async-done | bytes 262160 | tf_op jit(solution)/shard_map/while/body/eval_jaxpr/psum | solution.py:112
  1569.1 85.9 %all-reduce.7.cloned.1.call-done = f32[512,128]{1,0:T(8,128)} async-done(((f32[512,128]{1,0:T(8,128)}), f32[512,128]{1,0:T(8,128)}) %all-reduce.7.cloned.1.call-update) | async-done | bytes 262160 | tf_op jit(solution)/shard_map/while/body/eval_jaxpr/psum | solution.py:11
  1664.2 37.7 %all-reduce.9.cloned.1.call-done = f32[512,128]{1,0:T(8,128)} async-done(((f32[512,128]{1,0:T(8,128)}), f32[512,128]{1,0:T(8,128)}) %all-reduce.9.cloned.1.call-update) | async-done | bytes 262160 | tf_op jit(solution)/shard_map/while/body/eval_jaxpr/psum | solution.py:112
  1702.9 88.1 %all-reduce.7.cloned.1.call-done = f32[512,128]{1,0:T(8,128)} async-done(((f32[512,128]{1,0:T(8,128)}), f32[512,128]{1,0:T(8,128)}) %all-reduce.7.cloned.1.call-update) | async-done | bytes 262160 | tf_op jit(solution)/shard_map/while/body/eval_jaxpr/psum | solution.py:11
  1801.1 40.6 %all-reduce.9.cloned.1.call-done = f32[512,128]{1,0:T(8,128)} async-done(((f32[512,128]{1,0:T(8,128)}), f32[512,128]{1,0:T(8,128)}) %all-reduce.9.cloned.1.call-update) | async-done | bytes 262160 | tf_op jit(solution)/shard_map/while/body/eval_jaxpr/psum | solution.py:112
  1842.6 86.8 %all-reduce.7.cloned.1.call-done = f32[512,128]{1,0:T(8,128)} async-done(((f32[512,128]{1,0:T(8,128)}), f32[512,128]{1,0:T(8,128)}) %all-reduce.7.cloned.1.call-update) | async-done | bytes 262160 | tf_op jit(solution)/shard_map/while/body/eval_jaxpr/psum | solution.py:11
  1933.0 5.7 conditional.16
  1940.4 37.8 %all-reduce.9.cloned.1.call-done = f32[512,128]{1,0:T(8,128)} async-done(((f32[512,128]{1,0:T(8,128)}), f32[512,128]{1,0:T(8,128)}) %all-reduce.9.cloned.1.call-update) | async-done | bytes 262160 | tf_op jit(solution)/shard_map/while/body/eval_jaxpr/psum | solution.py:112
  1979.1 85.3 %all-reduce.7.cloned.1.call-done = f32[512,128]{1,0:T(8,128)} async-done(((f32[512,128]{1,0:T(8,128)}), f32[512,128]{1,0:T(8,128)}) %all-reduce.7.cloned.1.call-update) | async-done | bytes 262160 | tf_op jit(solution)/shard_map/while/body/eval_jaxpr/psum | solution.py:11
  2068.1 5.7 conditional.16
  2074.6 9.9 collective-permute-done
  2084.6 65.1 %conditional.15 = (f32[512,128]{1,0:T(8,128)S(1)}) conditional(s32[]{:T(128)} %convert_element_type.68, () %tuple.144, (s32[]{:T(128)}, s32[]{:T(128)}, f32[4,2,512,512]{2,3,0,1:T(8,128)}, s32[]{:T(128)}, pred[]{:T(512)}, /*index=5*/pred[]{:T(512)}, s32[]{:T(128)}, f32[2,512,128]{2,1,0:T(8,128)}, f32[512,128]{1,0:T(8,128)S(1)}, ...), branch_computations={%region_6.7_spmd, %region_7.8_spmd} | conditional | flops 252690464 | bytes 22546512 | solution.py:76
  2084.6 10.0 copy.8
  2095.9 10.6 while.27
  2106.5 40.1 %custom-call.5 = f32[4,128,128]{1,2,0:T(8,128)S(1)} custom-call(f32[4,128,128]{2,1,0:T(8,128)} %get-tuple-element.560), custom_call_target="InvertDiagBlocksLowerTriangular" | custom-call | tf_op jit(solution)/shard_map/while/body/eval_jaxpr/cond/branch_1_fun/triangular_solve/custom-call.1 | solution.py:72
  2151.5 48.9 %all-reduce.7.cloned.1.call-done = f32[512,128]{1,0:T(8,128)} async-done(((f32[512,128]{1,0:T(8,128)}), f32[512,128]{1,0:T(8,128)}) %all-reduce.7.cloned.1.call-update) | async-done | bytes 262160 | tf_op jit(solution)/shard_map/while/body/eval_jaxpr/psum | solution.py:11
  2201.4 11.0 fusion.55
  (350 shorter events, 182.1 us)
Async XLA Ops:
  7.2 2194.2 %copy-start = (f32[2,1,512,128]{3,2,1,0:T(8,128)S(1)}, f32[2,1,512,128]{3,2,1,0:T(8,128)}, u32[]{:S(2)}) copy-start(f32[2,1,512,128]{3,2,1,0:T(8,128)} %param.20) | copy-start | bytes 1572868
  7.2 145.9 %all-reduce.5.cloned.1.call-start = ((), (), s32[]{:S(2)}) async-start(), calls=%async_computation | async-start | bytes 524288 | tf_op jit(solution)/shard_map/psum | solution.py:11
  7.2 17.2 copy-start.3
  153.3 50.7 %all-reduce.9.cloned.1.call-start = ((), (), s32[]{:S(2)}) async-start(), calls=%async_computation.2 | async-start | bytes 524288 | tf_op jit(solution)/shard_map/while/body/eval_jaxpr/psum | solution.py:112
  153.4 9.1 collective-permute-start
  158.5 133.2 %all-reduce.7.cloned.1.call-start = ((), (), s32[]{:S(2)}) async-start(), calls=%async_computation.1 | async-start | bytes 524288 | tf_op jit(solution)/shard_map/while/body/eval_jaxpr/psum | solution.py:11
  291.7 48.7 %all-reduce.9.cloned.1.call-start = ((), (), s32[]{:S(2)}) async-start(), calls=%async_computation.2 | async-start | bytes 524288 | tf_op jit(solution)/shard_map/while/body/eval_jaxpr/psum | solution.py:112
  291.9 8.1 collective-permute-start
  296.0 130.7 %all-reduce.7.cloned.1.call-start = ((), (), s32[]{:S(2)}) async-start(), calls=%async_computation.1 | async-start | bytes 524288 | tf_op jit(solution)/shard_map/while/body/eval_jaxpr/psum | solution.py:11
  426.8 49.7 %all-reduce.9.cloned.1.call-start = ((), (), s32[]{:S(2)}) async-start(), calls=%async_computation.2 | async-start | bytes 524288 | tf_op jit(solution)/shard_map/while/body/eval_jaxpr/psum | solution.py:112
  426.9 8.1 collective-permute-start
  431.1 132.2 %all-reduce.7.cloned.1.call-start = ((), (), s32[]{:S(2)}) async-start(), calls=%async_computation.1 | async-start | bytes 524288 | tf_op jit(solution)/shard_map/while/body/eval_jaxpr/psum | solution.py:11
  564.3 46.0 %all-reduce.9.cloned.1.call-start = ((), (), s32[]{:S(2)}) async-start(), calls=%async_computation.2 | async-start | bytes 524288 | tf_op jit(solution)/shard_map/while/body/eval_jaxpr/psum | solution.py:112
  564.5 7.3 collective-permute-start
  567.7 131.6 %all-reduce.7.cloned.1.call-start = ((), (), s32[]{:S(2)}) async-start(), calls=%async_computation.1 | async-start | bytes 524288 | tf_op jit(solution)/shard_map/while/body/eval_jaxpr/psum | solution.py:11
  699.4 50.6 %all-reduce.9.cloned.1.call-start = ((), (), s32[]{:S(2)}) async-start(), calls=%async_computation.2 | async-start | bytes 524288 | tf_op jit(solution)/shard_map/while/body/eval_jaxpr/psum | solution.py:112
  699.5 9.1 collective-permute-start
  704.6 133.1 %all-reduce.7.cloned.1.call-start = ((), (), s32[]{:S(2)}) async-start(), calls=%async_computation.1 | async-start | bytes 524288 | tf_op jit(solution)/shard_map/while/body/eval_jaxpr/psum | solution.py:11
  837.8 48.7 %all-reduce.9.cloned.1.call-start = ((), (), s32[]{:S(2)}) async-start(), calls=%async_computation.2 | async-start | bytes 524288 | tf_op jit(solution)/shard_map/while/body/eval_jaxpr/psum | solution.py:112
  838.0 10.0 collective-permute-start
  847.8 125.0 %all-reduce.7.cloned.1.call-start = ((), (), s32[]{:S(2)}) async-start(), calls=%async_computation.1 | async-start | bytes 524288 | tf_op jit(solution)/shard_map/while/body/eval_jaxpr/psum | solution.py:11
  972.9 86.0 %all-reduce.9.cloned.1.call-start = ((), (), s32[]{:S(2)}) async-start(), calls=%async_computation.2 | async-start | bytes 524288 | tf_op jit(solution)/shard_map/while/body/eval_jaxpr/psum | solution.py:112
  973.0 19.9 collective-permute-start
  977.2 131.5 %all-reduce.7.cloned.1.call-start = ((), (), s32[]{:S(2)}) async-start(), calls=%async_computation.1 | async-start | bytes 524288 | tf_op jit(solution)/shard_map/while/body/eval_jaxpr/psum | solution.py:11
  1109.7 46.2 %all-reduce.9.cloned.1.call-start = ((), (), s32[]{:S(2)}) async-start(), calls=%async_computation.2 | async-start | bytes 524288 | tf_op jit(solution)/shard_map/while/body/eval_jaxpr/psum | solution.py:112
  1109.9 7.3 collective-permute-start
  1113.1 131.8 %all-reduce.7.cloned.1.call-start = ((), (), s32[]{:S(2)}) async-start(), calls=%async_computation.1 | async-start | bytes 524288 | tf_op jit(solution)/shard_map/while/body/eval_jaxpr/psum | solution.py:11
  1244.9 50.7 %all-reduce.9.cloned.1.call-start = ((), (), s32[]{:S(2)}) async-start(), calls=%async_computation.2 | async-start | bytes 524288 | tf_op jit(solution)/shard_map/while/body/eval_jaxpr/psum | solution.py:112
  1245.1 9.1 collective-permute-start
  1250.2 133.2 %all-reduce.7.cloned.1.call-start = ((), (), s32[]{:S(2)}) async-start(), calls=%async_computation.1 | async-start | bytes 524288 | tf_op jit(solution)/shard_map/while/body/eval_jaxpr/psum | solution.py:11
  1383.4 48.7 %all-reduce.9.cloned.1.call-start = ((), (), s32[]{:S(2)}) async-start(), calls=%async_computation.2 | async-start | bytes 524288 | tf_op jit(solution)/shard_map/while/body/eval_jaxpr/psum | solution.py:112
  1383.5 8.1 collective-permute-start
  1387.7 130.7 %all-reduce.7.cloned.1.call-start = ((), (), s32[]{:S(2)}) async-start(), calls=%async_computation.1 | async-start | bytes 524288 | tf_op jit(solution)/shard_map/while/body/eval_jaxpr/psum | solution.py:11
  1518.4 49.7 %all-reduce.9.cloned.1.call-start = ((), (), s32[]{:S(2)}) async-start(), calls=%async_computation.2 | async-start | bytes 524288 | tf_op jit(solution)/shard_map/while/body/eval_jaxpr/psum | solution.py:112
  1518.6 8.1 collective-permute-start
  1522.7 132.2 %all-reduce.7.cloned.1.call-start = ((), (), s32[]{:S(2)}) async-start(), calls=%async_computation.1 | async-start | bytes 524288 | tf_op jit(solution)/shard_map/while/body/eval_jaxpr/psum | solution.py:11
  1656.0 46.0 %all-reduce.9.cloned.1.call-start = ((), (), s32[]{:S(2)}) async-start(), calls=%async_computation.2 | async-start | bytes 524288 | tf_op jit(solution)/shard_map/while/body/eval_jaxpr/psum | solution.py:112
  1656.1 7.3 collective-permute-start
  1659.3 131.6 %all-reduce.7.cloned.1.call-start = ((), (), s32[]{:S(2)}) async-start(), calls=%async_computation.1 | async-start | bytes 524288 | tf_op jit(solution)/shard_map/while/body/eval_jaxpr/psum | solution.py:11
  1791.0 50.6 %all-reduce.9.cloned.1.call-start = ((), (), s32[]{:S(2)}) async-start(), calls=%async_computation.2 | async-start | bytes 524288 | tf_op jit(solution)/shard_map/while/body/eval_jaxpr/psum | solution.py:112
  1791.2 9.1 collective-permute-start
  1796.3 133.1 %all-reduce.7.cloned.1.call-start = ((), (), s32[]{:S(2)}) async-start(), calls=%async_computation.1 | async-start | bytes 524288 | tf_op jit(solution)/shard_map/while/body/eval_jaxpr/psum | solution.py:11
  1929.5 48.7 %all-reduce.9.cloned.1.call-start = ((), (), s32[]{:S(2)}) async-start(), calls=%async_computation.2 | async-start | bytes 524288 | tf_op jit(solution)/shard_map/while/body/eval_jaxpr/psum | solution.py:112
  1929.6 9.9 collective-permute-start
  1939.4 125.0 %all-reduce.7.cloned.1.call-start = ((), (), s32[]{:S(2)}) async-start(), calls=%async_computation.1 | async-start | bytes 524288 | tf_op jit(solution)/shard_map/while/body/eval_jaxpr/psum | solution.py:11
  2064.5 86.0 %all-reduce.9.cloned.1.call-start = ((), (), s32[]{:S(2)}) async-start(), calls=%async_computation.2 | async-start | bytes 524288 | tf_op jit(solution)/shard_map/while/body/eval_jaxpr/psum | solution.py:112
  2064.7 19.9 collective-permute-start
  2074.5 125.8 %all-reduce.7.cloned.1.call-start = ((), (), s32[]{:S(2)}) async-start(), calls=%async_computation.1 | async-start | bytes 524288 | tf_op jit(solution)/shard_map/while/body/eval_jaxpr/psum | solution.py:11
  (16 other events, 22.0 us)
Sparse Core Ops, SparseCore 0:
  35.2 117.8 all-reduce.4
  158.6 45.2 all-reduce.8
  207.6 84.0 all-reduce.6
  296.2 44.2 all-reduce.8
  343.9 82.7 all-reduce.6
  431.2 45.2 all-reduce.8
  480.1 83.1 all-reduce.6
  567.8 42.4 all-reduce.8
  614.0 85.3 all-reduce.6
  704.8 45.2 all-reduce.8
  753.7 84.0 all-reduce.6
  847.9 38.5 all-reduce.8
  890.2 82.6 all-reduce.6
  977.3 44.9 all-reduce.8
  1058.9 49.7 all-reduce.6
  1113.2 42.6 all-reduce.8
  1159.4 85.4 all-reduce.6
  1250.3 45.2 all-reduce.8
  1299.2 84.0 all-reduce.6
  1387.8 44.2 all-reduce.8
  1435.7 82.6 all-reduce.6
  1522.8 45.2 all-reduce.8
  1571.7 83.1 all-reduce.6
  1659.5 42.4 all-reduce.8
  1705.6 85.3 all-reduce.6
  1796.4 45.2 all-reduce.8
  1845.1 84.2 all-reduce.6
  1939.6 38.5 all-reduce.8
  1981.8 82.6 all-reduce.6
  2074.7 45.0 all-reduce.8
  2150.6 49.7 all-reduce.6
where the time goes:
time: 2220 us
  waiting for transfers between devices  1920 us (86%)
  other arithmetic  111 us (5%)
  local copies, waits for them, and re-layouts  84.6 us (4%)
  starting transfers between devices  53 us (2%)
  matrix products  32.1 us (1%)
    psum x16, waiting for transfers between devices, broadcast(): return lax.psum(jnp.where(mine, value, jnp.zeros_like(value)), axis)  1340 us
    psum x15, waiting for transfers between devices, sweep_step(): next_sum = lax.psum(next_partial, 'row')  512 us
    another operation x10, other arithmetic, solve_here(): lax.linalg.triangular_solve(diagonal, right_side, left_side=True, lower=T...  83 us
    ppermute x15, waiting for transfers between devices, from_behind(): lax.ppermute(value, axis, [(i, (i + by) % size) for i in range(size)])  68.5 us
    ppermute x15, starting transfers between devices, from_behind(): lax.ppermute(value, axis, [(i, (i + by) % size) for i in range(size)])  51.7 us
  transfers between devices with their start and end apart: 46, of which 42 were waited for; matrix products, arithmetic and copies ran while one was open for 8% of the time, Pallas kernels for 0%

commit v1 on v0

--- a/solution.py
+++ b/solution.py
@@ -109,7 +109,10 @@
         moved_term = from_behind(fresh_term, "row", -1)
         following = jnp.maximum(target - 1, 0)
         next_partial = column_partial(rhs_local, following, source)
-        next_sum = lax.psum(next_partial, "row")
+        n_dev, next_sum = (lax.axis_size("row"), next_partial)
+        for far in [1 << k for k in range(n_dev.bit_length() - 1)]:
+            swap = [(i_2, i_2 ^ far) for i_2 in range(n_dev)]
+            next_sum = next_sum + lax.ppermute(next_sum, "row", swap)
         carried = advance(target_block(target) - early_sum - moved_term, target, carried)
         return (carried, next_sum)
 

time: 2220 us -> 2300 us (1.036)
  starting transfers between devices: 53 us -> 99 us
  waiting for transfers between devices: 1920 us -> 1950 us
  other arithmetic: 111 us -> 139 us
  local copies, waits for them, and re-layouts: 84.6 us -> 60.8 us
    psum x15 -> x0, waiting for transfers between devices: 512 us -> none  [sweep_step(): next_sum = lax.psum(next_partial, 'row')]
    psum x16, waiting for transfers between devices: 1340 us -> 1830 us  [broadcast(): return lax.psum(jnp.where(mine, value, jnp.zeros_like(value)), axis)]
    ppermute x0 -> x30, starting transfers between devices: none -> 47.2 us  [sweep_step(): next_sum = next_sum + lax.ppermute(next_sum, 'row', swap)]
    ppermute x0 -> x30, waiting for transfers between devices: none -> 44.8 us  [sweep_step(): next_sum = next_sum + lax.ppermute(next_sum, 'row', swap)]
    add x0 -> x30, other arithmetic: none -> 26 us  [sweep_step(): next_sum = next_sum + lax.ppermute(next_sum, 'row', swap)]
    while x45 -> x15, local copies, waits for them, and re-layouts: 25 us -> 0.27 us
  transfers between devices with their start and end apart: 46 -> 61, of which waited for: 42 -> 43; matrix products, arithmetic and copies ran while one was open for 8% -> 8% of each run, Pallas kernels for 0% -> 0%
where the time goes in v1:
time: 2300 us
  waiting for transfers between devices  1950 us (85%)
  other arithmetic  139 us (6%)
  starting transfers between devices  99 us (4%)
  local copies, waits for them, and re-layouts  60.8 us (3%)
  matrix products  38.6 us (2%)
    psum x16, waiting for transfers between devices, broadcast(): return lax.psum(jnp.where(mine, value, jnp.zeros_like(value)), axis)  1830 us
    another operation x10, other arithmetic, solve_here(): lax.linalg.triangular_solve(diagonal, right_side, left_side=True, lower=T...  84.2 us
    ppermute x15, waiting for transfers between devices, from_behind(): lax.ppermute(value, axis, [(i, (i + by) % size) for i in range(size)])  74.7 us
    ppermute x15, starting transfers between devices, from_behind(): lax.ppermute(value, axis, [(i, (i + by) % size) for i in range(size)])  51.7 us
    ppermute x30, starting transfers between devices, sweep_step(): next_sum = next_sum + lax.ppermute(next_sum, 'row', swap)  47.2 us
  transfers between devices with their start and end apart: 61, of which 43 were waited for; matrix products, arithmetic and copies ran while one was open for 8% of the time, Pallas kernels for 0%

profile of v1, /device:TPU:0, one launch (start us, length us, event | category | flops | bytes accessed | tf_op | source)
XLA Modules:
  0.0 2300.6 jit_solution(567687843818260156)
XLA Ops:
  7.3 9.9 copy.12
  17.2 7.3 copy.11
  24.4 9.6 convert_select_fusion
  35.9 117.0 %all-reduce.4.cloned.1.call-done = f32[512,128]{1,0:T(8,128)} async-done(((f32[512,128]{1,0:T(8,128)}), f32[512,128]{1,0:T(8,128)}) %all-reduce.4.cloned.1.call-update) | async-done | bytes 262160 | tf_op jit(solution)/shard_map/psum | solution.py:11
  153.0 2130.2 %while.29 = (s32[]{:T(128)}, f32[4,512,128]{2,1,0:T(8,128)S(1)}, f32[512,128]{1,0:T(8,128)}, s32[]{:T(128)}, s32[]{:T(128)}, /*index=5*/f32[4,2,512,512]{2,3,0,1...) while((s32[]{:T(128)}, f32[4,512,128]{2,1,0:T(8,128)S(1)}, ...), condition=%wide.region_11.13_spmd.clone.clone.clone, body=%wide.region_3.12_spmd.clone.clone.clone.sunk | while | flops 2266611712 | bytes 56102800 | solution.py:119
  157.7 6.5 collective-permute-done
  170.4 125.8 %all-reduce.6.cloned.1.call-done = f32[512,128]{1,0:T(8,128)} async-done(((f32[512,128]{1,0:T(8,128)}), f32[512,128]{1,0:T(8,128)}) %all-reduce.6.cloned.1.call-update) | async-done | bytes 262160 | tf_op jit(solution)/shard_map/while/body/eval_jaxpr/psum | solution.py:11
  300.5 6.5 collective-permute-done
  314.4 122.0 %all-reduce.6.cloned.1.call-done = f32[512,128]{1,0:T(8,128)} async-done(((f32[512,128]{1,0:T(8,128)}), f32[512,128]{1,0:T(8,128)}) %all-reduce.6.cloned.1.call-update) | async-done | bytes 262160 | tf_op jit(solution)/shard_map/while/body/eval_jaxpr/psum | solution.py:11
  440.9 6.5 collective-permute-done
  453.8 124.8 %all-reduce.6.cloned.1.call-done = f32[512,128]{1,0:T(8,128)} async-done(((f32[512,128]{1,0:T(8,128)}), f32[512,128]{1,0:T(8,128)}) %all-reduce.6.cloned.1.call-update) | async-done | bytes 262160 | tf_op jit(solution)/shard_map/while/body/eval_jaxpr/psum | solution.py:11
  583.0 6.6 collective-permute-done
  595.9 123.9 %all-reduce.6.cloned.1.call-done = f32[512,128]{1,0:T(8,128)} async-done(((f32[512,128]{1,0:T(8,128)}), f32[512,128]{1,0:T(8,128)}) %all-reduce.6.cloned.1.call-update) | async-done | bytes 262160 | tf_op jit(solution)/shard_map/while/body/eval_jaxpr/psum | solution.py:11
  738.7 124.9 %all-reduce.6.cloned.1.call-done = f32[512,128]{1,0:T(8,128)} async-done(((f32[512,128]{1,0:T(8,128)}), f32[512,128]{1,0:T(8,128)}) %all-reduce.6.cloned.1.call-update) | async-done | bytes 262160 | tf_op jit(solution)/shard_map/while/body/eval_jaxpr/psum | solution.py:11
  867.8 5.7 conditional.19
  867.8 5.7 fusion.11
  875.3 4.7 collective-permute-done.1
  881.2 122.7 %all-reduce.6.cloned.1.call-done = f32[512,128]{1,0:T(8,128)} async-done(((f32[512,128]{1,0:T(8,128)}), f32[512,128]{1,0:T(8,128)}) %all-reduce.6.cloned.1.call-update) | async-done | bytes 262160 | tf_op jit(solution)/shard_map/while/body/eval_jaxpr/psum | solution.py:11
  1008.2 12.2 collective-permute-start.1
  1025.1 69.9 %conditional.18 = (f32[512,128]{1,0:T(8,128)S(1)}) conditional(s32[]{:T(128)} %convert_element_type.71, () %tuple.154, (s32[]{:T(128)}, s32[]{:T(128)}, f32[4,2,512,512]{2,3,0,1:T(8,128)}, s32[]{:T(128)}, pred[]{:T(512)}, /*index=5*/pred[]{:T(512)}, s32[]{:T(128)}, f32[2,512,128]{2,1,0:T(8,128)}, s32[]{:T(128)}, f32[512,128]{1,0:T(8,128)S(1)}, ...), branch_computations={%region_6.7_spmd, %region_7.8_spmd} | conditional | flops 252756000 | bytes 23857272 | solution.py:76
  1025.8 10.0 copy.8
  1037.1 10.5 while.28
  1047.6 40.7 %custom-call.6 = f32[4,128,128]{1,2,0:T(8,128)} custom-call(f32[4,128,128]{2,1,0:T(8,128)} %get-tuple-element.591), custom_call_target="InvertDiagBlocksLowerTriangular" | custom-call | tf_op jit(solution)/shard_map/while/body/eval_jaxpr/cond/branch_1_fun/triangular_solve/custom-call.1 | solution.py:72
  1096.8 48.8 %all-reduce.6.cloned.1.call-done = f32[512,128]{1,0:T(8,128)} async-done(((f32[512,128]{1,0:T(8,128)}), f32[512,128]{1,0:T(8,128)}) %all-reduce.6.cloned.1.call-update) | async-done | bytes 262160 | tf_op jit(solution)/shard_map/while/body/eval_jaxpr/psum | solution.py:11
  1150.0 6.6 collective-permute-done
  1162.9 124.2 %all-reduce.6.cloned.1.call-done = f32[512,128]{1,0:T(8,128)} async-done(((f32[512,128]{1,0:T(8,128)}), f32[512,128]{1,0:T(8,128)}) %all-reduce.6.cloned.1.call-update) | async-done | bytes 262160 | tf_op jit(solution)/shard_map/while/body/eval_jaxpr/psum | solution.py:11
  1292.4 6.5 collective-permute-done
  1305.1 125.8 %all-reduce.6.cloned.1.call-done = f32[512,128]{1,0:T(8,128)} async-done(((f32[512,128]{1,0:T(8,128)}), f32[512,128]{1,0:T(8,128)}) %all-reduce.6.cloned.1.call-update) | async-done | bytes 262160 | tf_op jit(solution)/shard_map/while/body/eval_jaxpr/psum | solution.py:11
  1435.3 6.5 collective-permute-done
  1449.2 122.0 %all-reduce.6.cloned.1.call-done = f32[512,128]{1,0:T(8,128)} async-done(((f32[512,128]{1,0:T(8,128)}), f32[512,128]{1,0:T(8,128)}) %all-reduce.6.cloned.1.call-update) | async-done | bytes 262160 | tf_op jit(solution)/shard_map/while/body/eval_jaxpr/psum | solution.py:11
  1575.6 6.5 collective-permute-done
  1588.6 124.8 %all-reduce.6.cloned.1.call-done = f32[512,128]{1,0:T(8,128)} async-done(((f32[512,128]{1,0:T(8,128)}), f32[512,128]{1,0:T(8,128)}) %all-reduce.6.cloned.1.call-update) | async-done | bytes 262160 | tf_op jit(solution)/shard_map/while/body/eval_jaxpr/psum | solution.py:11
  1717.7 6.6 collective-permute-done
  1730.7 124.0 %all-reduce.6.cloned.1.call-done = f32[512,128]{1,0:T(8,128)} async-done(((f32[512,128]{1,0:T(8,128)}), f32[512,128]{1,0:T(8,128)}) %all-reduce.6.cloned.1.call-update) | async-done | bytes 262160 | tf_op jit(solution)/shard_map/while/body/eval_jaxpr/psum | solution.py:11
  1873.5 124.9 %all-reduce.6.cloned.1.call-done = f32[512,128]{1,0:T(8,128)} async-done(((f32[512,128]{1,0:T(8,128)}), f32[512,128]{1,0:T(8,128)}) %all-reduce.6.cloned.1.call-update) | async-done | bytes 262160 | tf_op jit(solution)/shard_map/while/body/eval_jaxpr/psum | solution.py:11
  2002.6 5.7 conditional.19
  2002.6 5.7 fusion.11
  2010.1 4.7 collective-permute-done.1
  2016.1 122.7 %all-reduce.6.cloned.1.call-done = f32[512,128]{1,0:T(8,128)} async-done(((f32[512,128]{1,0:T(8,128)}), f32[512,128]{1,0:T(8,128)}) %all-reduce.6.cloned.1.call-update) | async-done | bytes 262160 | tf_op jit(solution)/shard_map/while/body/eval_jaxpr/psum | solution.py:11
  2143.0 5.7 conditional.19
  2143.0 5.7 fusion.11
  2148.7 12.2 collective-permute-start.1
  2160.9 69.9 %conditional.18 = (f32[512,128]{1,0:T(8,128)S(1)}) conditional(s32[]{:T(128)} %convert_element_type.71, () %tuple.154, (s32[]{:T(128)}, s32[]{:T(128)}, f32[4,2,512,512]{2,3,0,1:T(8,128)}, s32[]{:T(128)}, pred[]{:T(512)}, /*index=5*/pred[]{:T(512)}, s32[]{:T(128)}, f32[2,512,128]{2,1,0:T(8,128)}, s32[]{:T(128)}, f32[512,128]{1,0:T(8,128)S(1)}, ...), branch_computations={%region_6.7_spmd, %region_7.8_spmd} | conditional | flops 252756000 | bytes 23857272 | solution.py:76
  2161.7 10.0 copy.8
  2173.0 10.5 while.28
  2183.5 40.7 %custom-call.6 = f32[4,128,128]{1,2,0:T(8,128)} custom-call(f32[4,128,128]{2,1,0:T(8,128)} %get-tuple-element.591), custom_call_target="InvertDiagBlocksLowerTriangular" | custom-call | tf_op jit(solution)/shard_map/while/body/eval_jaxpr/cond/branch_1_fun/triangular_solve/custom-call.1 | solution.py:72
  2232.7 48.8 %all-reduce.6.cloned.1.call-done = f32[512,128]{1,0:T(8,128)} async-done(((f32[512,128]{1,0:T(8,128)}), f32[512,128]{1,0:T(8,128)}) %all-reduce.6.cloned.1.call-update) | async-done | bytes 262160 | tf_op jit(solution)/shard_map/while/body/eval_jaxpr/psum | solution.py:11
  2283.2 10.9 fusion.55
  (369 shorter events, 209.3 us)
Async XLA Ops:
  7.2 145.7 %all-reduce.4.cloned.1.call-start = ((), (), s32[]{:S(2)}) async-start(), calls=%async_computation | async-start | bytes 524288 | tf_op jit(solution)/shard_map/psum | solution.py:11
  153.0 143.1 %all-reduce.6.cloned.1.call-start = ((), (), s32[]{:S(2)}) async-start(), calls=%async_computation.1 | async-start | bytes 524288 | tf_op jit(solution)/shard_map/while/body/eval_jaxpr/psum | solution.py:11
  153.2 11.0 collective-permute-start
  157.5 10.3 collective-permute-start.1
  168.9 127.3 %collective-permute-start.2 = (f32[512,128]{1,0:T(8,128)S(1)}, f32[512,128]{1,0:T(8,128)S(1)}, u32[]{:S(2)}, u32[]{:S(2)}) collective-permute-start(f32[512,128]{1,0:T(8,128)S(1)} %add.341), channel_id=1, source_target_pairs={{0,16},{8,24},{16,0},{24,8},{1,17},{9,25},{17,1},{25,9},{2,18},{10... | collective-permute-start | bytes 786440 | tf_op jit(solution)/shard_map/while/body/eval_jaxpr/ppermute | solution.py:115
  297.0 139.5 %all-reduce.6.cloned.1.call-start = ((), (), s32[]{:S(2)}) async-start(), calls=%async_computation.1 | async-start | bytes 524288 | tf_op jit(solution)/shard_map/while/body/eval_jaxpr/psum | solution.py:11
  300.4 10.3 collective-permute-start.1
  311.7 124.8 %collective-permute-start.2 = (f32[512,128]{1,0:T(8,128)S(1)}, f32[512,128]{1,0:T(8,128)S(1)}, u32[]{:S(2)}, u32[]{:S(2)}) collective-permute-start(f32[512,128]{1,0:T(8,128)S(1)} %add.341), channel_id=1, source_target_pairs={{0,16},{8,24},{16,0},{24,8},{1,17},{9,25},{17,1},{25,9},{2,18},{10... | collective-permute-start | bytes 786440 | tf_op jit(solution)/shard_map/while/body/eval_jaxpr/ppermute | solution.py:115
  437.3 141.3 %all-reduce.6.cloned.1.call-start = ((), (), s32[]{:S(2)}) async-start(), calls=%async_computation.1 | async-start | bytes 524288 | tf_op jit(solution)/shard_map/while/body/eval_jaxpr/psum | solution.py:11
  440.7 10.3 collective-permute-start.1
  452.1 127.5 %collective-permute-start.2 = (f32[512,128]{1,0:T(8,128)S(1)}, f32[512,128]{1,0:T(8,128)S(1)}, u32[]{:S(2)}, u32[]{:S(2)}) collective-permute-start(f32[512,128]{1,0:T(8,128)S(1)} %add.341), channel_id=1, source_target_pairs={{0,16},{8,24},{16,0},{24,8},{1,17},{9,25},{17,1},{25,9},{2,18},{10... | collective-permute-start | bytes 786440 | tf_op jit(solution)/shard_map/while/body/eval_jaxpr/ppermute | solution.py:115
  580.3 139.5 %all-reduce.6.cloned.1.call-start = ((), (), s32[]{:S(2)}) async-start(), calls=%async_computation.1 | async-start | bytes 524288 | tf_op jit(solution)/shard_map/while/body/eval_jaxpr/psum | solution.py:11
  582.8 10.6 collective-permute-start.1
  594.4 125.5 %collective-permute-start.2 = (f32[512,128]{1,0:T(8,128)S(1)}, f32[512,128]{1,0:T(8,128)S(1)}, u32[]{:S(2)}, u32[]{:S(2)}) collective-permute-start(f32[512,128]{1,0:T(8,128)S(1)} %add.341), channel_id=1, source_target_pairs={{0,16},{8,24},{16,0},{24,8},{1,17},{9,25},{17,1},{25,9},{2,18},{10... | collective-permute-start | bytes 786440 | tf_op jit(solution)/shard_map/while/body/eval_jaxpr/ppermute | solution.py:115
  720.7 142.9 %all-reduce.6.cloned.1.call-start = ((), (), s32[]{:S(2)}) async-start(), calls=%async_computation.1 | async-start | bytes 524288 | tf_op jit(solution)/shard_map/while/body/eval_jaxpr/psum | solution.py:11
  725.0 10.2 collective-permute-start.1
  736.2 127.4 %collective-permute-start.2 = (f32[512,128]{1,0:T(8,128)S(1)}, f32[512,128]{1,0:T(8,128)S(1)}, u32[]{:S(2)}, u32[]{:S(2)}) collective-permute-start(f32[512,128]{1,0:T(8,128)S(1)} %add.341), channel_id=1, source_target_pairs={{0,16},{8,24},{16,0},{24,8},{1,17},{9,25},{17,1},{25,9},{2,18},{10... | collective-permute-start | bytes 786440 | tf_op jit(solution)/shard_map/while/body/eval_jaxpr/ppermute | solution.py:115
  864.4 139.5 %all-reduce.6.cloned.1.call-start = ((), (), s32[]{:S(2)}) async-start(), calls=%async_computation.1 | async-start | bytes 524288 | tf_op jit(solution)/shard_map/while/body/eval_jaxpr/psum | solution.py:11
  881.0 122.9 %collective-permute-start.2 = (f32[512,128]{1,0:T(8,128)S(1)}, f32[512,128]{1,0:T(8,128)S(1)}, u32[]{:S(2)}, u32[]{:S(2)}) collective-permute-start(f32[512,128]{1,0:T(8,128)S(1)} %add.341), channel_id=1, source_target_pairs={{0,16},{8,24},{16,0},{24,8},{1,17},{9,25},{17,1},{25,9},{2,18},{10... | collective-permute-start | bytes 786440 | tf_op jit(solution)/shard_map/while/body/eval_jaxpr/ppermute | solution.py:115
  1004.7 140.9 %all-reduce.6.cloned.1.call-start = ((), (), s32[]{:S(2)}) async-start(), calls=%async_computation.1 | async-start | bytes 524288 | tf_op jit(solution)/shard_map/while/body/eval_jaxpr/psum | solution.py:11
  1004.8 20.3 collective-permute-start
  1008.2 87.5 %collective-permute-start.1 = (f32[512,128]{1,0:T(8,128)S(1)}, f32[512,128]{1,0:T(8,128)}, u32[]{:S(2)}, u32[]{:S(2)}) collective-permute-start(f32[512,128]{1,0:T(8,128)S(1)} %get-tuple-element.852), channel_id=1, source_target_pairs={{0,8},{8,0},{16,24},{24,16},{1,9},{9,1},{17,25},{25,17},{2,10},{10... | collective-permute-start | bytes 786440 | tf_op jit(solution)/shard_map/while/body/eval_jaxpr/ppermute | solution.py:115
  1096.7 49.9 %collective-permute-start.2 = (f32[512,128]{1,0:T(8,128)S(1)}, f32[512,128]{1,0:T(8,128)S(1)}, u32[]{:S(2)}, u32[]{:S(2)}) collective-permute-start(f32[512,128]{1,0:T(8,128)S(1)} %add.341), channel_id=1, source_target_pairs={{0,16},{8,24},{16,0},{24,8},{1,17},{9,25},{17,1},{25,9},{2,18},{10... | collective-permute-start | bytes 786440 | tf_op jit(solution)/shard_map/while/body/eval_jaxpr/ppermute | solution.py:115
  1147.4 139.8 %all-reduce.6.cloned.1.call-start = ((), (), s32[]{:S(2)}) async-start(), calls=%async_computation.1 | async-start | bytes 524288 | tf_op jit(solution)/shard_map/while/body/eval_jaxpr/psum | solution.py:11
  1149.9 10.6 collective-permute-start.1
  1161.4 125.8 %collective-permute-start.2 = (f32[512,128]{1,0:T(8,128)S(1)}, f32[512,128]{1,0:T(8,128)S(1)}, u32[]{:S(2)}, u32[]{:S(2)}) collective-permute-start(f32[512,128]{1,0:T(8,128)S(1)} %add.341), channel_id=1, source_target_pairs={{0,16},{8,24},{16,0},{24,8},{1,17},{9,25},{17,1},{25,9},{2,18},{10... | collective-permute-start | bytes 786440 | tf_op jit(solution)/shard_map/while/body/eval_jaxpr/ppermute | solution.py:115
  1287.9 143.0 %all-reduce.6.cloned.1.call-start = ((), (), s32[]{:S(2)}) async-start(), calls=%async_computation.1 | async-start | bytes 524288 | tf_op jit(solution)/shard_map/while/body/eval_jaxpr/psum | solution.py:11
  1287.9 11.0 collective-permute-start
  1292.3 10.3 collective-permute-start.1
  1303.6 127.3 %collective-permute-start.2 = (f32[512,128]{1,0:T(8,128)S(1)}, f32[512,128]{1,0:T(8,128)S(1)}, u32[]{:S(2)}, u32[]{:S(2)}) collective-permute-start(f32[512,128]{1,0:T(8,128)S(1)} %add.341), channel_id=1, source_target_pairs={{0,16},{8,24},{16,0},{24,8},{1,17},{9,25},{17,1},{25,9},{2,18},{10... | collective-permute-start | bytes 786440 | tf_op jit(solution)/shard_map/while/body/eval_jaxpr/ppermute | solution.py:115
  1431.7 139.5 %all-reduce.6.cloned.1.call-start = ((), (), s32[]{:S(2)}) async-start(), calls=%async_computation.1 | async-start | bytes 524288 | tf_op jit(solution)/shard_map/while/body/eval_jaxpr/psum | solution.py:11
  1435.2 10.3 collective-permute-start.1
  1446.5 124.8 %collective-permute-start.2 = (f32[512,128]{1,0:T(8,128)S(1)}, f32[512,128]{1,0:T(8,128)S(1)}, u32[]{:S(2)}, u32[]{:S(2)}) collective-permute-start(f32[512,128]{1,0:T(8,128)S(1)} %add.341), channel_id=1, source_target_pairs={{0,16},{8,24},{16,0},{24,8},{1,17},{9,25},{17,1},{25,9},{2,18},{10... | collective-permute-start | bytes 786440 | tf_op jit(solution)/shard_map/while/body/eval_jaxpr/ppermute | solution.py:115
  1572.1 141.3 %all-reduce.6.cloned.1.call-start = ((), (), s32[]{:S(2)}) async-start(), calls=%async_computation.1 | async-start | bytes 524288 | tf_op jit(solution)/shard_map/while/body/eval_jaxpr/psum | solution.py:11
  1575.5 10.3 collective-permute-start.1
  1586.8 127.5 %collective-permute-start.2 = (f32[512,128]{1,0:T(8,128)S(1)}, f32[512,128]{1,0:T(8,128)S(1)}, u32[]{:S(2)}, u32[]{:S(2)}) collective-permute-start(f32[512,128]{1,0:T(8,128)S(1)} %add.341), channel_id=1, source_target_pairs={{0,16},{8,24},{16,0},{24,8},{1,17},{9,25},{17,1},{25,9},{2,18},{10... | collective-permute-start | bytes 786440 | tf_op jit(solution)/shard_map/while/body/eval_jaxpr/ppermute | solution.py:115
  1715.1 139.5 %all-reduce.6.cloned.1.call-start = ((), (), s32[]{:S(2)}) async-start(), calls=%async_computation.1 | async-start | bytes 524288 | tf_op jit(solution)/shard_map/while/body/eval_jaxpr/psum | solution.py:11
  1717.6 10.6 collective-permute-start.1
  1729.1 125.6 %collective-permute-start.2 = (f32[512,128]{1,0:T(8,128)S(1)}, f32[512,128]{1,0:T(8,128)S(1)}, u32[]{:S(2)}, u32[]{:S(2)}) collective-permute-start(f32[512,128]{1,0:T(8,128)S(1)} %add.341), channel_id=1, source_target_pairs={{0,16},{8,24},{16,0},{24,8},{1,17},{9,25},{17,1},{25,9},{2,18},{10... | collective-permute-start | bytes 786440 | tf_op jit(solution)/shard_map/while/body/eval_jaxpr/ppermute | solution.py:115
  1855.5 143.0 %all-reduce.6.cloned.1.call-start = ((), (), s32[]{:S(2)}) async-start(), calls=%async_computation.1 | async-start | bytes 524288 | tf_op jit(solution)/shard_map/while/body/eval_jaxpr/psum | solution.py:11
  1859.8 10.2 collective-permute-start.1
  1871.0 127.4 %collective-permute-start.2 = (f32[512,128]{1,0:T(8,128)S(1)}, f32[512,128]{1,0:T(8,128)S(1)}, u32[]{:S(2)}, u32[]{:S(2)}) collective-permute-start(f32[512,128]{1,0:T(8,128)S(1)} %add.341), channel_id=1, source_target_pairs={{0,16},{8,24},{16,0},{24,8},{1,17},{9,25},{17,1},{25,9},{2,18},{10... | collective-permute-start | bytes 786440 | tf_op jit(solution)/shard_map/while/body/eval_jaxpr/ppermute | solution.py:115
  1999.2 139.5 %all-reduce.6.cloned.1.call-start = ((), (), s32[]{:S(2)}) async-start(), calls=%async_computation.1 | async-start | bytes 524288 | tf_op jit(solution)/shard_map/while/body/eval_jaxpr/psum | solution.py:11
  2015.9 122.9 %collective-permute-start.2 = (f32[512,128]{1,0:T(8,128)S(1)}, f32[512,128]{1,0:T(8,128)S(1)}, u32[]{:S(2)}, u32[]{:S(2)}) collective-permute-start(f32[512,128]{1,0:T(8,128)S(1)} %add.341), channel_id=1, source_target_pairs={{0,16},{8,24},{16,0},{24,8},{1,17},{9,25},{17,1},{25,9},{2,18},{10... | collective-permute-start | bytes 786440 | tf_op jit(solution)/shard_map/while/body/eval_jaxpr/ppermute | solution.py:115
  2139.6 141.9 %all-reduce.6.cloned.1.call-start = ((), (), s32[]{:S(2)}) async-start(), calls=%async_computation.1 | async-start | bytes 524288 | tf_op jit(solution)/shard_map/while/body/eval_jaxpr/psum | solution.py:11
  2139.6 21.3 collective-permute-start
  2148.7 82.9 %collective-permute-start.1 = (f32[512,128]{1,0:T(8,128)S(1)}, f32[512,128]{1,0:T(8,128)}, u32[]{:S(2)}, u32[]{:S(2)}) collective-permute-start(f32[512,128]{1,0:T(8,128)S(1)} %get-tuple-element.852), channel_id=1, source_target_pairs={{0,8},{8,0},{16,24},{24,16},{1,9},{9,1},{17,25},{25,17},{2,10},{10... | collective-permute-start | bytes 786440 | tf_op jit(solution)/shard_map/while/body/eval_jaxpr/ppermute | solution.py:115
  2232.5 49.9 %collective-permute-start.2 = (f32[512,128]{1,0:T(8,128)S(1)}, f32[512,128]{1,0:T(8,128)S(1)}, u32[]{:S(2)}, u32[]{:S(2)}) collective-permute-start(f32[512,128]{1,0:T(8,128)S(1)} %add.341), channel_id=1, source_target_pairs={{0,16},{8,24},{16,0},{24,8},{1,17},{9,25},{17,1},{25,9},{2,18},{10... | collective-permute-start | bytes 786440 | tf_op jit(solution)/shard_map/while/body/eval_jaxpr/ppermute | solution.py:115
  (18 other events, 2425.0 us)
Sparse Core Ops, SparseCore 0:
  35.1 117.7 all-reduce.3
  165.1 130.9 all-reduce.5
  308.0 128.4 all-reduce.5
  448.3 130.1 all-reduce.5
  590.5 129.2 all-reduce.5
  730.7 132.8 all-reduce.5
  875.4 128.4 all-reduce.5
  1095.8 49.7 all-reduce.5
  1157.6 129.5 all-reduce.5
  1299.9 130.9 all-reduce.5
  1442.8 128.4 all-reduce.5
  1583.1 130.1 all-reduce.5
  1725.3 129.3 all-reduce.5
  1865.5 132.8 all-reduce.5
  2010.3 128.4 all-reduce.5
  2231.7 49.7 all-reduce.5
